TPU v7x, 32 devices: a whole 2x2x4 slice. The times are simulated.
32 devices in a mesh: dp: 4 (over z), mp: 8 (over y, x, core).
Axes of the slice: x: 2, y: 2, z: 4, core: 2. Of those that a mesh axis runs over, the one named last changes fastest.
Arguments:
- inputs: bfloat16 [197, 49152], P(None, ('dp', 'mp')), may hold values from -6 to 6
- cotangent: bfloat16 [197, 49152], P(None, ('dp', 'mp')), may hold values from -1.1953125 to 1.1953125
- w_in: bfloat16 [768, 3072], P('dp', 'mp'), may hold values from -0.21875 to 0.21875
- w_out: bfloat16 [3072, 768], P('mp', 'dp'), may hold values from -0.109375 to 0.109375
- prec_in: float32 [768, 3072], P('dp', 'mp'), may hold values from 0.1 to 2
- prec_out: float32 [3072, 768], P('mp', 'dp'), may hold values from 0.1 to 2
Outputs:
- new_prec_in: float32 [768, 3072], P('dp', 'mp')
- new_prec_out: float32 [3072, 768], P('mp', 'dp')
- new_w_in: float32 [768, 3072], P('dp', 'mp')
- new_w_out: float32 [3072, 768], P('mp', 'dp')
All inputs are finite; a program needn't handle non-finite values.
Results may differ from a plain program's by a relative error of at most 0.0028.
Values may be sent and summed in bfloat16 or wider, within the bound.
A program may use at most 64 MiB of HBM per device.

v0:
```python
import jax
import jax.numpy as jnp
from jax import lax
from jax.sharding import PartitionSpec as P

D = 768
SEQ = 197


def gelu_tanh(v):
    return jax.nn.gelu(v, approximate=True)


def per_device(inputs, cotangent, w_in, w_out, prec_in, prec_out):
    w_in_full, w_out_full = (
        lax.all_gather(w_in, "dp", axis=0, tiled=True),
        lax.all_gather(w_out, "dp", axis=1, tiled=True),
    )
    whole = lax.all_gather(inputs, "mp", axis=1, tiled=True)
    rows3 = whole.reshape(SEQ, -1, D)
    images = rows3.shape[1]
    pre = jnp.einsum("snd,dh->snh", rows3, w_in_full, preferred_element_type=jnp.float32)
    act = gelu_tanh(pre).astype(jnp.bfloat16)
    cot_whole = lax.all_gather(cotangent, "mp", axis=1, tiled=True)
    cot3 = cot_whole.reshape(SEQ, images, D)
    back = jnp.einsum("snd,hd->snh", cot3, w_out_full, preferred_element_type=jnp.float32)
    per_out = jnp.einsum("snh,snd->nhd", act, cot3, preferred_element_type=jnp.float32)
    sum_out = jnp.sum(per_out, 0)
    sq_out = jnp.sum(per_out * per_out, 0)
    delta = jax.vjp(gelu_tanh, pre)[1](back)[0].astype(jnp.bfloat16)
    rows_again = lax.all_gather(inputs, "mp", axis=1, tiled=True).reshape(SEQ, images, D)
    per_in = jnp.einsum("snd,snh->ndh", rows_again, delta, preferred_element_type=jnp.float32)
    sum_in = jnp.sum(per_in, 0)
    sq_in = jnp.sum(per_in * per_in, 0)
    sum_in, sq_in = (
        lax.psum_scatter(sum_in, "dp", scatter_dimension=0, tiled=True),
        lax.psum_scatter(sq_in, "dp", scatter_dimension=0, tiled=True),
    )
    sum_out, sq_out = (
        lax.psum_scatter(sum_out, "dp", scatter_dimension=1, tiled=True),
        lax.psum_scatter(sq_out, "dp", scatter_dimension=1, tiled=True),
    )
    scale = 1.0 / (images * lax.axis_size("dp"))
    new_prec_in = 0.6 * prec_in + 0.4 * sq_in * scale
    new_prec_out = 0.6 * prec_out + 0.4 * sq_out * scale
    w_in_own = w_in.astype(jnp.float32)
    w_out_own = w_out.astype(jnp.float32)
    new_w_in = w_in_own - 1.0 * (sum_in * scale + 0.1 * w_in_own) / (new_prec_in + 0.1)
    new_w_out = w_out_own - 1.0 * (sum_out * scale + 0.1 * w_out_own) / (new_prec_out + 0.1)
    return (new_prec_in, new_prec_out, new_w_in, new_w_out)


def solution(mesh):
    placed = (
        P(None, ("dp", "mp")),
        P(None, ("dp", "mp")),
        P("dp", "mp"),
        P("mp", "dp"),
        P("dp", "mp"),
        P("mp", "dp"),
    )
    return jax.shard_map(
        per_device,
        mesh=mesh,
        in_specs=placed,
        out_specs=(P("dp", "mp"), P("mp", "dp"), P("dp", "mp"), P("mp", "dp")),
        check_vma=False,
    )
```

profile of v0, /device:TPU:0, one launch (start us, length us, event | category | flops | bytes accessed | tf_op | source)
XLA Modules:
  0.0 244.7 jit_solution(8754437066115192813)
XLA Ops:
  8.7 18.5 %all_gather.16 = bf16[768,384]{1,0:T(8,128)(2,1)S(1)} all-gather(bf16[192,384]{1,0:T(8,128)(2,1)} %param.8), channel_id=1, replica_groups=mesh['dp'=4,'mp'=8] {'dp'}, dimensions={0}, use_global_device_ids=true | all-gather | bytes 737280 | tf_op jit(solution)/shard_map/all_gather | solution.py:16
  27.2 16.3 %all_gather.14 = bf16[384,768]{0,1:T(8,128)(2,1)S(1)} all-gather(bf16[384,192]{0,1:T(8,128)(2,1)} %param.9), channel_id=1, replica_groups=mesh['dp'=4,'mp'=8] {'dp'}, dimensions={1}, use_global_device_ids=true | all-gather | bytes 737280 | tf_op jit(solution)/shard_map/all_gather | solution.py:17
  43.5 8.7 %all-gather.5.cloned.1.call-done = bf16[197,12288]{1,0:T(8,128)(2,1)} async-done(((bf16[197,1536]{1,0:T(8,128)(2,1)}), bf16[197,12288]{1,0:T(8,128)(2,1)}) %all-gather.5.cloned.1.call-update) | async-done | bytes 4841488 | tf_op jit(solution)/shard_map/all_gather | solution.py:31
  52.2 3.8 %copy.47 = bf16[25,8,16,768]{3,2,1,0:T(8,128)(2,1)S(1)} copy(bf16[25,8,16,768]{3,1,2,0:T(8,128)(2,1)} %bitcast.30) | data formatting | bytes 9830400
  56.0 2.5 %slice.1 = bf16[197,16,768]{2,1,0:T(8,128)(2,1)} slice(bf16[200,16,768]{2,1,0:T(8,128)(2,1)S(1)} %bitcast.27), slice={[0:197], [0:16], [0:768]} | slice | bytes 9682944 | tf_op jit(solution)/shard_map/reshape | solution.py:31
  58.5 5.6 %multiply_convert_fusion = (bf16[197,16,384]{2,1,0:T(8,128)(2,1)}, f32[197,16,384]{2,1,0:T(8,128)}) fusion(bf16[768,384]{1,0:T(8,128)(2,1)S(1)} %all_gather.16, bf16[200,16,768]{2,1,0:T(8,128)(2,1)S(1)} %bitcast.28), kind=kOutput, calls=%fused_computation.17 | convolution fusion | flops 1870018560 | bytes 12693504 | tf_op jit(solution)/shard_map/snd,dh->snh/dot_general | solution.py:22
  64.2 29.6 %all-gather.3.cloned.1.call-done = bf16[197,12288]{1,0:T(8,128)(2,1)} async-done(((bf16[197,1536]{1,0:T(8,128)(2,1)}), bf16[197,12288]{1,0:T(8,128)(2,1)}) %all-gather.3.cloned.1.call-update) | async-done | bytes 4841488 | tf_op jit(solution)/shard_map/all_gather | solution.py:24
  93.8 3.9 %copy.46 = bf16[25,8,16,768]{3,2,1,0:T(8,128)(2,1)S(1)} copy(bf16[25,8,16,768]{3,1,2,0:T(8,128)(2,1)} %bitcast.29) | data formatting | bytes 9830400
  97.7 2.2 copy-done
  99.9 5.4 %fusion.11 = bf16[197,16,384]{2,1,0:T(8,128)(2,1)S(1)} fusion(f32[197,16,384]{2,1,0:T(8,128)S(1)} %copy-done.5, bf16[384,768]{0,1:T(8,128)(2,1)S(1)} %all_gather.14, bf16[200,16,768]{2,1,0:T(8,128)(2,1)S(1)} %bitcast.25), kind=kOutput, calls=%fused_computation.16 | convolution fusion | flops 1883332608 | bytes 12693504 | tf_op jit(solution)/shard_map/snd,hd->snh/dot_general | solution.py:26
  105.3 8.2 %bitcast_reduce_fusion = (f32[768,384]{0,1:T(8,128)S(1)}, f32[768,384]{0,1:T(8,128)S(1)}) fusion(bf16[197,16,768]{2,1,0:T(8,128)(2,1)S(1)} %bitcast.32, bf16[197,16,384]{2,1,0:T(8,128)(2,1)S(1)} %fusion.11), kind=kOutput, calls=%fused_computation | convolution fusion | flops 1872691200 | bytes 9621504 | tf_op jit(solution)/shard_map/snd,snh->ndh/dot_general | solution.py:32
  113.5 1.4 copy.38
  115.0 1.4 copy.42
  116.7 2.8 %slice = bf16[197,16,768]{2,1,0:T(8,128)(2,1)S(1)} slice(bf16[200,16,768]{2,1,0:T(8,128)(2,1)} %bitcast.26), slice={[0:197], [0:16], [0:768]} | slice | bytes 9682944 | tf_op jit(solution)/shard_map/reshape | solution.py:25
  119.8 8.2 %fusion.23 = (f32[384,768]{1,0:T(8,128)S(1)}, f32[384,768]{1,0:T(8,128)S(1)}) fusion(bf16[197,16,768]{2,1,0:T(8,128)(2,1)S(1)} %slice, bf16[197,16,384]{2,1,0:T(8,128)(2,1)S(1)} %copy-done.6), kind=kOutput, calls=%fused_computation.35 | convolution fusion | flops 1872691200 | bytes 9621504 | tf_op jit(solution)/shard_map/snh,snd->nhd/dot_general | solution.py:27
  128.1 1.4 copy.40
  129.6 1.4 copy.44
  131.7 12.8 %reduce-scatter.13.cloned.1.call-done = f32[192,384]{1,0:T(8,128)} async-done(((f32[768,384]{1,0:T(8,128)}), f32[192,384]{1,0:T(8,128)}) %reduce-scatter.13.cloned.1.call-update) | async-done | bytes 294928
  144.5 1.1 copy.39
  145.6 29.0 %reduce-scatter.17.cloned.1.call-done = f32[192,384]{1,0:T(8,128)} async-done(((f32[768,384]{1,0:T(8,128)}), f32[192,384]{1,0:T(8,128)}) %reduce-scatter.17.cloned.1.call-update) | async-done | bytes 294928
  174.6 1.1 copy.43
  177.6 27.1 %reduce-scatter.15.cloned.1.call-done = f32[192,384]{1,0:T(8,128)} async-done(((f32[768,384]{1,0:T(8,128)}), f32[192,384]{1,0:T(8,128)}) %reduce-scatter.15.cloned.1.call-update) | async-done | bytes 294928
  204.7 1.1 copy.41
  205.8 29.0 %reduce-scatter.19.cloned.1.call-done = f32[192,384]{1,0:T(8,128)} async-done(((f32[768,384]{1,0:T(8,128)}), f32[192,384]{1,0:T(8,128)}) %reduce-scatter.19.cloned.1.call-update) | async-done | bytes 294928
  (41 shorter events, 7.7 us)
Async XLA Ops:
  7.2 45.1 %all-gather.5.cloned.1.call-start = ((), (), s32[]{:S(2)}) async-start(), calls=%async_computation.5 | async-start | bytes 5529600 | tf_op jit(solution)/shard_map/all_gather | solution.py:31
  7.9 85.9 %all-gather.3.cloned.1.call-start = ((), (), s32[]{:S(2)}) async-start(), calls=%async_computation.4 | async-start | bytes 5529600 | tf_op jit(solution)/shard_map/all_gather | solution.py:24
  8.6 135.8 %reduce-scatter.13.cloned.1.call-start = ((), (), s32[]{:S(2)}) async-start(), calls=%async_computation.6 | async-start | bytes 1474560
  93.8 6.1 %copy-start.5 = (f32[197,16,384]{2,1,0:T(8,128)S(1)}, f32[197,16,384]{2,1,0:T(8,128)}, u32[]{:S(2)}) copy-start(f32[197,16,384]{2,1,0:T(8,128)} %get-tuple-element.21) | copy-start | bytes 14524420
  93.8 11.5 %slice-start = ((s8[4841472]{0:T(1024)(128)(4,1)}), s8[4194304]{0:T(1024)(128)(4,1)S(1)}, s32[]{:S(2)}) async-start(s8[4841472]{0:T(1024)(128)(4,1)} %bitcast.31), calls=%async_computation.10 | async-start | bytes 8388608
  97.7 2.2 copy-start
  99.9 5.4 %slice-start.1 = ((s8[4841472]{0:T(1024)(128)(4,1)}), s8[647168]{0:T(1024)(128)(4,1)S(1)}, s32[]{:S(2)}) async-start(s8[4841472]{0:T(1024)(128)(4,1)} %bitcast.31), calls=%async_computation.11 | async-start | bytes 1294336
  115.0 59.6 %reduce-scatter.17.cloned.1.call-start = ((), (), s32[]{:S(2)}) async-start(), calls=%async_computation.8 | async-start | bytes 1474560
  116.5 88.2 %reduce-scatter.15.cloned.1.call-start = ((), (), s32[]{:S(2)}) async-start(), calls=%async_computation.7 | async-start | bytes 1474560
  116.7 3.1 %copy-start.6 = (bf16[197,16,384]{2,1,0:T(8,128)(2,1)S(1)}, bf16[197,16,384]{2,1,0:T(8,128)(2,1)}, u32[]{:S(2)}) copy-start(bf16[197,16,384]{2,1,0:T(8,128)(2,1)} %get-tuple-element.20) | copy-start | bytes 7262212
  128.0 2.9 %copy-start.1 = (bf16[192,384]{1,0:T(8,128)(2,1)S(1)}, bf16[192,384]{1,0:T(8,128)(2,1)}, u32[]{:S(2)}) copy-start(bf16[192,384]{1,0:T(8,128)(2,1)} %param.8) | copy-start | bytes 442372
  128.1 3.1 %copy-start.2 = (bf16[384,192]{0,1:T(8,128)(2,1)S(1)}, bf16[384,192]{0,1:T(8,128)(2,1)}, u32[]{:S(2)}) copy-start(bf16[384,192]{0,1:T(8,128)(2,1)} %param.9) | copy-start | bytes 442372
  128.1 3.2 %copy-start.3 = (f32[192,384]{1,0:T(8,128)S(1)}, f32[192,384]{1,0:T(8,128)}, u32[]{:S(2)}) copy-start(f32[192,384]{1,0:T(8,128)} %param.10) | copy-start | bytes 884740
  128.1 3.4 %copy-start.4 = (f32[384,192]{0,1:T(8,128)S(1)}, f32[384,192]{0,1:T(8,128)}, u32[]{:S(2)}) copy-start(f32[384,192]{0,1:T(8,128)} %param.11) | copy-start | bytes 884740
  129.5 105.3 %reduce-scatter.19.cloned.1.call-start = ((), (), s32[]{:S(2)}) async-start(), calls=%async_computation.9 | async-start | bytes 1474560
Sparse Core Ops, SparseCore 0:
  9.9 42.3 all-gather.4
  54.1 39.5 all-gather.2
  115.1 29.3 reduce-scatter.12
  146.6 27.9 reduce-scatter.16
  176.7 27.9 reduce-scatter.14
  206.9 27.9 reduce-scatter.18
where the time goes:
time: 245 us
  waiting for transfers between devices  138 us (56%)
  blocking collectives  34.8 us (14%)
  local copies, waits for them, and re-layouts  29.7 us (12%)
  matrix products  27.4 us (11%)
  between operations  14.3 us (6%)
    unnamed x10, waiting for transfers between devices  99.3 us
    all_gather x1, waiting for transfers between devices, per_device(): cot_whole = lax.all_gather(cotangent, 'mp', axis=1, tiled=True)  29.6 us
    unnamed x36, local copies, waits for them, and re-layouts  24.4 us
    all_gather x1, blocking collectives, per_device(): lax.all_gather(w_in, 'dp', axis=0, tiled=True)  18.5 us
    all_gather x1, blocking collectives, per_device(): lax.all_gather(w_out, 'dp', axis=1, tiled=True)  16.3 us
    all_gather x1, waiting for transfers between devices, per_device(): lax.all_gather(inputs, 'mp', axis=1, tiled=True).reshape(SEQ, images, D)  8.74 us
    dot_general x1, matrix products, per_device(): jnp.einsum('snh,snd->nhd', act, cot3, preferred_element_type=jnp.float32)  8.2 us
    dot_general x1, matrix products, per_device(): jnp.einsum('snd,snh->ndh', rows_again, delta, preferred_element_type=jnp....  8.2 us
  transfers between devices with their start and end apart: 6, of which 6 were waited for; matrix products, arithmetic and copies ran while one was open for 13% of the time, Pallas kernels for 0%

commit v1 on v0

--- a/solution.py
+++ b/solution.py
@@ -2,9 +2,15 @@
 import jax.numpy as jnp
 from jax import lax
 from jax.sharding import PartitionSpec as P
+from jax.lax import all_gather
 
 D = 768
 SEQ = 197
+
+
+def replace_edges(target, across):
+    outer = all_gather(target, across)
+    return jnp.concatenate(outer, 1)
 
 
 def gelu_tanh(v):
@@ -21,7 +27,7 @@
     images = rows3.shape[1]
     pre = jnp.einsum("snd,dh->snh", rows3, w_in_full, preferred_element_type=jnp.float32)
     act = gelu_tanh(pre).astype(jnp.bfloat16)
-    cot_whole = lax.all_gather(cotangent, "mp", axis=1, tiled=True)
+    cot_whole = replace_edges(cotangent, "mp")
     cot3 = cot_whole.reshape(SEQ, images, D)
     back = jnp.einsum("snd,hd->snh", cot3, w_out_full, preferred_element_type=jnp.float32)
     per_out = jnp.einsum("snh,snd->nhd", act, cot3, preferred_element_type=jnp.float32)

time: 245 us -> 257 us (1.049)
  matrix products: 27.4 us -> 32.5 us
  local copies, waits for them, and re-layouts: 29.7 us -> 34.8 us
    another operation x0 -> x1, local copies, waits for them, and re-layouts: none -> 8.16 us  [per_device(): cot3 = cot_whole.reshape(SEQ, images, D)]
    unnamed x36 -> x29, local copies, waits for them, and re-layouts: 24.4 us -> 18 us
    reshape x1, local copies, waits for them, and re-layouts: 2.83 us -> 6.09 us  [replace_edges(): return jnp.concatenate(outer, 1)]
    dot_general x1, matrix products: 5.38 us -> 8.37 us  [per_device(): jnp.einsum('snd,hd->snh', cot3, w_out_full, preferred_element_type=jnp.fl...]
where the time goes in v1:
time: 257 us; the launch traced here: 256 us
  waiting for transfers between devices  139 us (54%)
  blocking collectives  34.8 us (14%)
  local copies, waits for them, and re-layouts  34.8 us (14%)
  matrix products  32.5 us (13%)
  between operations  14.3 us (6%)
    unnamed x10, waiting for transfers between devices  101 us
    all_gather x1, waiting for transfers between devices, replace_edges(): outer = all_gather(target, across)  29.6 us
    all_gather x1, blocking collectives, per_device(): lax.all_gather(w_in, 'dp', axis=0, tiled=True)  18.5 us
    unnamed x29, local copies, waits for them, and re-layouts  18 us
    all_gather x1, blocking collectives, per_device(): lax.all_gather(w_out, 'dp', axis=1, tiled=True)  16.3 us
    dot_general x1, matrix products, per_device(): jnp.einsum('snh,snd->nhd', act, cot3, preferred_element_type=jnp.float32)  10.1 us
    all_gather x1, waiting for transfers between devices, per_device(): lax.all_gather(inputs, 'mp', axis=1, tiled=True).reshape(SEQ, images, D)  8.74 us
    dot_general x1, matrix products, per_device(): jnp.einsum('snd,snh->ndh', rows_again, delta, preferred_element_type=jnp....  8.38 us
  transfers between devices with their start and end apart: 6, of which 6 were waited for; matrix products, arithmetic and copies ran while one was open for 13% of the time, Pallas kernels for 0%

profile of v1, /device:TPU:0, one launch (start us, length us, event | category | flops | bytes accessed | tf_op | source)
XLA Modules:
  0.0 256.0 jit_solution(14900853392925463815)
XLA Ops:
  8.7 18.5 %all_gather.20 = bf16[768,384]{1,0:T(8,128)(2,1)S(1)} all-gather(bf16[192,384]{1,0:T(8,128)(2,1)} %param.8), channel_id=1, replica_groups=mesh['dp'=4,'mp'=8] {'dp'}, dimensions={0}, use_global_device_ids=true | all-gather | bytes 737280 | tf_op jit(solution)/shard_map/all_gather | solution.py:22
  27.2 16.3 %all_gather.18 = bf16[384,768]{0,1:T(8,128)(2,1)S(1)} all-gather(bf16[384,192]{0,1:T(8,128)(2,1)} %param.9), channel_id=1, replica_groups=mesh['dp'=4,'mp'=8] {'dp'}, dimensions={1}, use_global_device_ids=true | all-gather | bytes 737280 | tf_op jit(solution)/shard_map/all_gather | solution.py:23
  43.5 8.7 %all-gather.5.cloned.1.call-done = bf16[197,12288]{1,0:T(8,128)(2,1)} async-done(((bf16[197,1536]{1,0:T(8,128)(2,1)}), bf16[197,12288]{1,0:T(8,128)(2,1)}) %all-gather.5.cloned.1.call-update) | async-done | bytes 4841488 | tf_op jit(solution)/shard_map/all_gather | solution.py:37
  52.2 3.8 %copy.49 = bf16[25,8,16,768]{3,2,1,0:T(8,128)(2,1)S(1)} copy(bf16[25,8,16,768]{3,1,2,0:T(8,128)(2,1)} %bitcast.28) | data formatting | bytes 9830400
  56.0 2.5 slice
  58.6 5.7 %multiply_convert_fusion = (bf16[197,16,384]{2,1,0:T(8,128)(2,1)}, f32[197,16,384]{2,1,0:T(8,128)}) fusion(bf16[768,384]{1,0:T(8,128)(2,1)S(1)} %all_gather.20, bf16[200,16,768]{2,1,0:T(8,128)(2,1)S(1)} %bitcast.26), kind=kOutput, calls=%fused_computation.17 | convolution fusion | flops 1870018560 | bytes 12693504 | tf_op jit(solution)/shard_map/snd,dh->snh/dot_general | solution.py:28
  64.2 29.6 %all-gather.7.cloned.1.call-done = bf16[8,197,1536]{2,1,0:T(8,128)(2,1)} async-done(((bf16[1,197,1536]{2,1,0:T(8,128)(2,1)}), bf16[8,197,1536]{2,1,0:T(8,128)(2,1)}) %all-gather.7.cloned.1.call-update) | async-done | bytes 4841488 | tf_op jit(solution)/shard_map/all_gather | solution.py:12
  93.8 6.1 %copy.29 = bf16[197,8,1536]{2,1,0:T(8,128)(2,1)} copy(bf16[197,8,1536]{2,0,1:T(8,128)(2,1)} %bitcast.27) | data formatting | bytes 9682944 | tf_op jit(solution)/shard_map/reshape | solution.py:13
  99.9 8.2 %reshape_reshape.3 = bf16[197,16,768]{2,1,0:T(8,128)(2,1)} reshape(bf16[197,8,1536]{2,1,0:T(8,128)(2,1)} %copy.29) | data formatting | bytes 9682944 | tf_op jit(solution)/shard_map/reshape;reshape | solution.py:31
  108.0 8.4 %fusion.11 = bf16[197,16,384]{2,1,0:T(8,128)(2,1)S(1)} fusion(f32[197,16,384]{2,1,0:T(8,128)} %get-tuple-element.21, bf16[197,16,768]{2,1,0:T(8,128)(2,1)} %reshape_reshape.3, bf16[384,768]{0,1:T(8,128)(2,1)S(1)} %all_gather.18), kind=kOutput, calls=%fused_computation.16 | convolution fusion | flops 1883332608 | bytes 12693504 | tf_op jit(solution)/shard_map/snd,hd->snh/dot_general | solution.py:32
  116.4 8.4 %bitcast_reduce_fusion = (f32[768,384]{0,1:T(8,128)S(1)}, f32[768,384]{0,1:T(8,128)S(1)}) fusion(bf16[197,16,768]{2,1,0:T(8,128)(2,1)S(1)} %bitcast.30, bf16[197,16,384]{2,1,0:T(8,128)(2,1)S(1)} %fusion.11), kind=kOutput, calls=%fused_computation | convolution fusion | flops 1872691200 | bytes 9621504 | tf_op jit(solution)/shard_map/snd,snh->ndh/dot_general | solution.py:38
  124.8 1.4 copy.41
  126.5 1.4 copy.45
  128.0 10.1 %fusion.22 = (f32[384,768]{1,0:T(8,128)S(1)}, f32[384,768]{1,0:T(8,128)S(1)}) fusion(bf16[197,16,768]{2,1,0:T(8,128)(2,1)} %reshape_reshape.3, bf16[197,16,384]{2,1,0:T(8,128)(2,1)} %get-tuple-element.20), kind=kOutput, calls=%fused_computation.34 | convolution fusion | flops 1872691200 | bytes 9621504 | tf_op jit(solution)/shard_map/snh,snd->nhd/dot_general | solution.py:33
  138.1 1.4 copy.43
  139.6 1.4 copy.47
  141.7 14.0 %reduce-scatter.13.cloned.1.call-done = f32[192,384]{1,0:T(8,128)} async-done(((f32[768,384]{1,0:T(8,128)}), f32[192,384]{1,0:T(8,128)}) %reduce-scatter.13.cloned.1.call-update) | async-done | bytes 294928
  155.7 1.1 copy.42
  156.9 29.0 %reduce-scatter.17.cloned.1.call-done = f32[192,384]{1,0:T(8,128)} async-done(((f32[768,384]{1,0:T(8,128)}), f32[192,384]{1,0:T(8,128)}) %reduce-scatter.17.cloned.1.call-update) | async-done | bytes 294928
  185.9 1.1 copy.46
  188.9 27.1 %reduce-scatter.15.cloned.1.call-done = f32[192,384]{1,0:T(8,128)} async-done(((f32[768,384]{1,0:T(8,128)}), f32[192,384]{1,0:T(8,128)}) %reduce-scatter.15.cloned.1.call-update) | async-done | bytes 294928
  216.0 1.1 copy.44
  217.1 29.0 %reduce-scatter.19.cloned.1.call-done = f32[192,384]{1,0:T(8,128)} async-done(((f32[768,384]{1,0:T(8,128)}), f32[192,384]{1,0:T(8,128)}) %reduce-scatter.19.cloned.1.call-update) | async-done | bytes 294928
  246.1 1.1 copy.48
  (35 shorter events, 6.3 us)
Async XLA Ops:
  7.2 45.1 %all-gather.5.cloned.1.call-start = ((), (), s32[]{:S(2)}) async-start(), calls=%async_computation.4 | async-start | bytes 5529600 | tf_op jit(solution)/shard_map/all_gather | solution.py:37
  7.9 85.9 %all-gather.7.cloned.1.call-start = ((), (), s32[]{:S(2)}) async-start(), calls=%async_computation.5 | async-start | bytes 5529600 | tf_op jit(solution)/shard_map/all_gather | solution.py:12
  8.6 147.1 %reduce-scatter.13.cloned.1.call-start = ((), (), s32[]{:S(2)}) async-start(), calls=%async_computation.6 | async-start | bytes 1474560
  99.9 16.5 %slice-start = ((s8[4841472]{0:T(1024)(128)(4,1)}), s8[647168]{0:T(1024)(128)(4,1)S(1)}, s32[]{:S(2)}) async-start(s8[4841472]{0:T(1024)(128)(4,1)} %bitcast.29), calls=%async_computation.10 | async-start | bytes 1294336
  108.0 8.4 %slice-start.1 = ((s8[4841472]{0:T(1024)(128)(4,1)}), s8[4194304]{0:T(1024)(128)(4,1)S(1)}, s32[]{:S(2)}) async-start(s8[4841472]{0:T(1024)(128)(4,1)} %bitcast.29), calls=%async_computation.11 | async-start | bytes 8388608
  126.3 59.6 %reduce-scatter.17.cloned.1.call-start = ((), (), s32[]{:S(2)}) async-start(), calls=%async_computation.8 | async-start | bytes 1474560
  127.9 88.1 %reduce-scatter.15.cloned.1.call-start = ((), (), s32[]{:S(2)}) async-start(), calls=%async_computation.7 | async-start | bytes 1474560
  138.1 2.9 %copy-start = (bf16[192,384]{1,0:T(8,128)(2,1)S(1)}, bf16[192,384]{1,0:T(8,128)(2,1)}, u32[]{:S(2)}) copy-start(bf16[192,384]{1,0:T(8,128)(2,1)} %param.8) | copy-start | bytes 442372
  138.1 3.1 %copy-start.1 = (bf16[384,192]{0,1:T(8,128)(2,1)S(1)}, bf16[384,192]{0,1:T(8,128)(2,1)}, u32[]{:S(2)}) copy-start(bf16[384,192]{0,1:T(8,128)(2,1)} %param.9) | copy-start | bytes 442372
  138.1 3.2 %copy-start.2 = (f32[192,384]{1,0:T(8,128)S(1)}, f32[192,384]{1,0:T(8,128)}, u32[]{:S(2)}) copy-start(f32[192,384]{1,0:T(8,128)} %param.10) | copy-start | bytes 884740
  138.1 3.4 %copy-start.3 = (f32[384,192]{0,1:T(8,128)S(1)}, f32[384,192]{0,1:T(8,128)}, u32[]{:S(2)}) copy-start(f32[384,192]{0,1:T(8,128)} %param.11) | copy-start | bytes 884740
  139.6 106.6 %reduce-scatter.19.cloned.1.call-start = ((), (), s32[]{:S(2)}) async-start(), calls=%async_computation.9 | async-start | bytes 1474560
Sparse Core Ops, SparseCore 0:
  9.9 42.3 all-gather.4
  54.1 39.5 all-gather.6
  126.4 29.3 reduce-scatter.12
  157.9 27.9 reduce-scatter.16
  188.0 27.9 reduce-scatter.14
  218.2 27.9 reduce-scatter.18
